TPU v7x, 128 devices: a whole 4x4x4 slice. The times are simulated.
128 devices in a mesh: dp: 8 (over z, core), mp: 16 (over y, x).
Axes of the slice: x: 4, y: 4, z: 4, core: 2. Of those that a mesh axis runs over, the one named last changes fastest.
Arguments:
- crop_hidden: bfloat16 [8, 1536, 8192], P(None, 'dp', 'mp'), may hold values from -15 to 15
- projector_weight: bfloat16 [8192, 8192], P('mp'), may hold values from -0.21213203 to 0.21213203
- pairing: int32 [8, 1536], P(None, 'dp'), may hold values from 0 to 191, as said below
Outputs:
- embeddings: float32 [8192, 8, 1536], P('mp', 'dp')
- loss_terms: float32 [4], replicated
Inputs may be any that keep to these rules, and one draw needn't show every extreme that they name: Each aligned block of 192 entries of a row of pairing is a permutation of 0 to 191.
All inputs are finite; a program needn't handle non-finite values.
Results may differ from a plain program's by a relative error of at most 0.0003.
Values may be sent and summed in bfloat16 or wider, within the bound.
No kernel may reach another device: no remote copies, remote signals or barrier semaphores. Data moves between devices by JAX's collectives and lax.ppermute only.
A program may use at most 128 MiB of HBM per device.

v0:
```python
import functools
import jax
import jax.numpy as jnp
from jax import lax
from jax.sharding import Mesh
from jax.sharding import PartitionSpec as P

MP = ("mp_0", "mp_1")
DP = ("dp_0", "dp_1")
DP_MP = ("dp_0", "dp_1", "mp_0", "mp_1")
highest = lax.Precision.HIGHEST
epsilon = 0.0001


def by_axis(x, axes):
    return functools.reduce(lax.psum, axes, x)


def local(crop_hidden, projector_weight, pairing):
    crop_count, local_rows, width_part = crop_hidden.shape
    features = projector_weight.shape[1]
    total_rows = crop_count * local_rows
    column_block = lax.all_to_all(projector_weight, MP, split_axis=1, concat_axis=0, tiled=True)
    shards = lax.all_gather(crop_hidden, MP, axis=2, tiled=True)
    flat_piece = shards.reshape(total_rows, shards.shape[2])
    embedded = lax.dot_general(
        column_block, flat_piece, (((0,), (1,)), ((), ())), preferred_element_type=jnp.float32
    )
    feature_part = embedded.shape[0]
    by_crop = embedded.reshape(feature_part, crop_count, local_rows)
    onehot = (pairing[:, :, None] == jnp.arange(local_rows, dtype=jnp.int32)[None, None, :]).astype(
        jnp.float32
    )
    aligned = jnp.einsum("jcr,cri->jci", by_crop, onehot, precision=highest)
    invariance = 0.0
    for anchor in range(2):
        differ = aligned - aligned[:, anchor : anchor + 1, :]
        invariance = invariance + jnp.sum(differ * differ)
    owned_block = lax.all_to_all(by_crop, DP, split_axis=1, concat_axis=2, tiled=True)
    batch_rows = owned_block.shape[2]
    column_mean = jnp.mean(owned_block, axis=2, keepdims=True)
    centered = owned_block - column_mean
    variance = jnp.sum(centered * centered, axis=2) / (batch_rows - 1)
    hinge_sum = jnp.sum(jax.nn.relu(1.0 - jnp.sqrt(variance + epsilon)))
    diagonal_sq = jnp.sum(variance * variance)
    gram_scale = 1.0 / ((batch_rows - 1) * (batch_rows - 1))
    partial_gram = jnp.einsum("jcr,jcs->crs", centered, centered, precision=highest)
    gram_block = lax.psum(partial_gram.astype(jnp.bfloat16), MP).astype(jnp.float32)
    frobenius = jnp.where(
        lax.axis_index(MP) == 0, jnp.sum(gram_block * gram_block) * gram_scale, 0.0
    )
    totals = (
        by_axis(invariance, DP_MP),
        by_axis(hinge_sum, DP_MP),
        by_axis(frobenius - diagonal_sq, DP_MP),
    )
    invariance_loss = totals[0] / (2 * (crop_count - 1) * batch_rows * features)
    variance_loss = totals[1] / (crop_count * features)
    covariance_loss = totals[2] / (crop_count * features)
    total_loss = 25.0 * invariance_loss + 25.0 * variance_loss + covariance_loss
    loss_terms = jnp.stack([invariance_loss, variance_loss, covariance_loss, total_loss])
    return (owned_block, loss_terms)


def solution(mesh):
    torus = Mesh(mesh.devices.reshape(4, 2, 4, 4), ("dp_0", "dp_1", "mp_0", "mp_1"))
    placed = (P(None, DP, MP), P(MP, None), P(None, DP))
    return jax.shard_map(
        local, mesh=torus, in_specs=placed, out_specs=(P(MP, DP, None), P()), check_vma=False
    )
```

profile of v0, /device:TPU:0, one launch (start us, length us, event | category | flops | bytes accessed | tf_op | source)
XLA Modules:
  0.0 498.9 jit_solution(17605152332946094416)
XLA Ops:
  7.2 0.0 all-gather.2.cloned.1.call-start
  7.2 0.7 all-gather.2.cloned.1.call-update
  7.9 0.0 all-reduce.6.cloned.1.call-start
  7.9 7.5 %copy.9 = bf16[64,16,8,512]{3,2,0,1:T(8,128)(2,1)} copy(bf16[64,16,8,512]{3,2,1,0:T(8,128)(2,1)} %bitcast.30) | data formatting | bytes 16777216 | tf_op jit(solution)/shard_map/all_to_all | solution.py:23
  15.4 128.3 %all_to_all.31 = bf16[512,16,512]{2,0,1:T(8,128)(2,1)} all-to-all(bf16[512,16,512]{2,0,1:T(8,128)(2,1)} %bitcast.29), channel_id=1, replica_groups=mesh['dp_0'=4,'dp_1'=2,'mp_0'=4,'mp_1'=4] {'mp_0','mp_1'}, dimensions={1} | all-to-all | bytes 16777216 | tf_op jit(solution)/shard_map/all_to_all | solution.py:23
  143.8 117.0 %all-gather.2.cloned.1.call-done = bf16[8,192,8192]{2,1,0:T(8,128)(2,1)} async-done(((bf16[8,192,512]{2,1,0:T(8,128)(2,1)}), bf16[8,192,8192]{2,1,0:T(8,128)(2,1)}) %all-gather.2.cloned.1.call-update) | async-done | bytes 25165840 | tf_op jit(solution)/shard_map/all_gather | solution.py:24
  260.8 18.9 %fusion.2 = f32[512,8,192]{0,2,1:T(8,128)S(1)} fusion(bf16[8192,512,1]{1,0,2:T(8,128)(2,1)} %bitcast.31, bf16[8,192,8192]{2,1,0:T(8,128)(2,1)} %all-gather.2.cloned.1.call-done), kind=kOutput, calls=%fused_computation.17 | convolution fusion | flops 12884901888 | bytes 36700160 | tf_op jit(solution)/shard_map/dot_general | solution.py:26
  279.7 0.0 copy-start
  279.7 1.7 copy-done
  281.3 42.7 %all_to_all.32 = f32[512,8,192]{0,2,1:T(8,128)S(1)} all-to-all(f32[512,8,192]{0,2,1:T(8,128)S(1)} %fusion.2), channel_id=1, replica_groups=mesh['dp_0'=4,'dp_1'=2,'mp_0'=4,'mp_1'=4] {'dp_0','dp_1'}, dimensions={1} | all-to-all | bytes 6291456 | tf_op jit(solution)/shard_map/all_to_all | solution.py:39
  324.0 0.3 reduce_sum.65
  324.3 0.6 multiply_reduce_fusion.1
  324.8 16.8 %fusion = bf16[1,1536,1536]{2,1,0:T(8,128)(2,1)} fusion(f32[512,1536]{0,1:T(8,128)S(1)} %bitcast.32), kind=kOutput, calls=%fused_computation.3 | convolution fusion | flops 14497873920 | bytes 7864320 | tf_op jit(solution)/shard_map/jcr,jcs->crs/dot_general | solution.py:47
  341.6 0.0 copy-start.1
  341.6 0.0 all-reduce.6.cloned.1.call-update
  341.6 0.7 copy-done.1
  342.3 3.9 convolution_bitcast_fusion
  346.2 0.1 slice_bitcast_fusion.1
  346.2 2.0 multiply_reduce_fusion.2
  349.5 5.4 %copy.6 = f32[512,1,1536]{2,1,0:T(1,128)} copy(f32[512,1,1536]{0,2,1:T(8,128)S(1)} %bitcast.28) | data formatting | bytes 6291456
  354.9 0.7 multiply_reduce_fusion.4
  355.6 91.4 %all-reduce.6.cloned.1.call-done = bf16[1,1536,1536]{2,1,0:T(8,128)(2,1)} async-done(((bf16[1,1536,1536]{2,1,0:T(8,128)(2,1)}), bf16[1,1536,1536]{2,1,0:T(8,128)(2,1)}) %all-reduce.6.cloned.1.call-update) | async-done | bytes 4718608 | tf_op jit(solution)/shard_map/psum | solution.py:48
  447.0 5.3 %multiply_reduce_fusion = f32[]{:T(128)} fusion(bf16[1,1536,1536]{2,1,0:T(8,128)(2,1)} %all-reduce.6.cloned.1.call-done), kind=kLoop, calls=%fused_computation | loop fusion | flops 7077887 | bytes 4718596 | tf_op jit(solution)/shard_map/reduce_sum | solution.py:50
  453.5 11.3 %all-reduce.2 = (f32[]{:T(128)}, f32[]{:T(128)}, f32[]{:T(128)}) all-reduce(f32[]{:T(128)S(6)} %add.47, f32[]{:T(128)} %get-tuple-element.7, f32[]{:T(128)S(6)} %sub.61), channel_id=1, replica_groups=mesh['dp_0'=4,'dp_1'=2,'mp_0'=4,'mp_1'=4] {'dp_0'}, use_global_device_ids=true, to_apply=%region_2.0 | all-reduce | flops 3 | bytes 24 | tf_op jit(solution)/shard_map/psum | solution.py:16
  464.8 3.2 all-reduce.3
  467.9 11.0 %all-reduce.1 = (f32[]{:T(128)}, f32[]{:T(128)}, f32[]{:T(128)}) all-reduce(f32[]{:T(128)} %get-tuple-element.17, f32[]{:T(128)} %get-tuple-element.18, f32[]{:T(128)} %get-tuple-element.19), channel_id=1, replica_groups=mesh['dp_0'=4,'dp_1'=2,'mp_0'=4,'mp_1'=4] {'mp_0'}, use_global_device_ids=true, to_apply=%region_4.5 | all-reduce | flops 3 | bytes 24 | tf_op jit(solution)/shard_map/psum | solution.py:16
  478.9 9.4 %all-reduce = (f32[]{:T(128)}, f32[]{:T(128)}, f32[]{:T(128)}) all-reduce(f32[]{:T(128)} %get-tuple-element.11, f32[]{:T(128)} %get-tuple-element.12, f32[]{:T(128)} %get-tuple-element.13), channel_id=1, replica_groups=mesh['dp_0'=4,'dp_1'=2,'mp_0'=4,'mp_1'=4] {'mp_1'}, use_global_device_ids=true, to_apply=%region_5.6 | all-reduce | flops 3 | bytes 24 | tf_op jit(solution)/shard_map/psum | solution.py:16
  491.5 0.6 pad_maximum_fusion
  (1 shorter events, 0.0 us)
Async XLA Ops:
  7.2 253.6 %all-gather.2.cloned.1.call-start = ((), (), s32[]{:S(2)}) async-start(), calls=%async_computation.2 | async-start | bytes 26738688 | tf_op jit(solution)/shard_map/all_gather | solution.py:24
  7.9 439.1 %all-reduce.6.cloned.1.call-start = ((), (), s32[]{:S(2)}) async-start(), calls=%async_computation.3 | async-start | bytes 9437184 | tf_op jit(solution)/shard_map/psum | solution.py:48
  279.7 1.7 copy-start
  341.6 0.7 copy-start.1
Sparse Core Ops, SparseCore 0:
  10.1 250.6 all-gather.1
  341.7 105.2 all-reduce.5
where the time goes:
time: 499 us
  waiting for transfers between devices  209 us (42%)
  blocking collectives  206 us (41%)
  matrix products  39.5 us (8%)
  between operations  19.8 us (4%)
  local copies, waits for them, and re-layouts  15.3 us (3%)
  other arithmetic  9.4 us (2%)
    all_to_all x1, blocking collectives, local(): lax.all_to_all(projector_weight, MP, split_axis=1, concat_axis=0, tiled=T...  128 us
    all_gather x1, waiting for transfers between devices, local(): shards = lax.all_gather(crop_hidden, MP, axis=2, tiled=True)  117 us
    psum x1, waiting for transfers between devices, local(): lax.psum(partial_gram.astype(jnp.bfloat16), MP).astype(jnp.float32)  91.4 us
    all_to_all x1, blocking collectives, local(): lax.all_to_all(by_crop, DP, split_axis=1, concat_axis=2, tiled=True)  42.7 us
    psum x4, blocking collectives, by_axis(): return functools.reduce(lax.psum, axes, x)  34.8 us
    dot_general x1, matrix products, local(): lax.dot_general(column_block, flat_piece, (((0,), (1,)), ((), ())), prefe...  18.9 us
    dot_general x1, matrix products, local(): jnp.einsum('jcr,jcs->crs', centered, centered, precision=highest)  16.8 us
  transfers between devices with their start and end apart: 2, of which 2 were waited for; matrix products, arithmetic and copies ran while one was open for 4% of the time, Pallas kernels for 0%

commit v1 on v0

--- a/solution.py
+++ b/solution.py
@@ -10,6 +10,7 @@
 DP_MP = ("dp_0", "dp_1", "mp_0", "mp_1")
 highest = lax.Precision.HIGHEST
 epsilon = 0.0001
+files_pack = lambda u: jnp.sum(lax.all_gather(u, MP), 0)
 
 
 def by_axis(x, axes):
@@ -45,7 +46,7 @@
     diagonal_sq = jnp.sum(variance * variance)
     gram_scale = 1.0 / ((batch_rows - 1) * (batch_rows - 1))
     partial_gram = jnp.einsum("jcr,jcs->crs", centered, centered, precision=highest)
-    gram_block = lax.psum(partial_gram.astype(jnp.bfloat16), MP).astype(jnp.float32)
+    gram_block = files_pack(partial_gram.astype(jnp.bfloat16)).astype(jnp.float32)
     frobenius = jnp.where(
         lax.axis_index(MP) == 0, jnp.sum(gram_block * gram_block) * gram_scale, 0.0
     )

time: 499 us -> 830 us (1.66)
  waiting for transfers between devices: 209 us -> 512 us
  other arithmetic: 9.4 us -> 36.5 us
    all_gather x0 -> x1, waiting for transfers between devices: none -> 395 us  [files_pack = lambda u: jnp.sum(lax.all_gather(u, MP), 0)]
    psum x1 -> x0, waiting for transfers between devices: 91.4 us -> none  [local(): lax.psum(partial_gram.astype(jnp.bfloat16), MP).astype(jnp.float32)]
    reduce_sum x0 -> x1, other arithmetic: none -> 26.9 us  [files_pack = lambda u: jnp.sum(lax.all_gather(u, MP), 0)]
  transfers between devices with their start and end apart: 2 -> 2, of which waited for: 2 -> 2; matrix products, arithmetic and copies ran while one was open for 4% -> 2% of each run, Pallas kernels for 0% -> 0%
where the time goes in v1:
time: 830 us
  waiting for transfers between devices  512 us (62%)
  blocking collectives  206 us (25%)
  matrix products  39.6 us (5%)
  other arithmetic  36.5 us (4%)
  between operations  20 us (2%)
  local copies, waits for them, and re-layouts  15.3 us (2%)
    all_gather x1, waiting for transfers between devices, files_pack = lambda u: jnp.sum(lax.all_gather(u, MP), 0)  395 us
    all_to_all x1, blocking collectives, local(): lax.all_to_all(projector_weight, MP, split_axis=1, concat_axis=0, tiled=T...  128 us
    all_gather x1, waiting for transfers between devices, local(): shards = lax.all_gather(crop_hidden, MP, axis=2, tiled=True)  117 us
    all_to_all x1, blocking collectives, local(): lax.all_to_all(by_crop, DP, split_axis=1, concat_axis=2, tiled=True)  42.7 us
    psum x4, blocking collectives, by_axis(): return functools.reduce(lax.psum, axes, x)  34.8 us
    reduce_sum x1, other arithmetic, files_pack = lambda u: jnp.sum(lax.all_gather(u, MP), 0)  26.9 us
    dot_general x1, matrix products, local(): lax.dot_general(column_block, flat_piece, (((0,), (1,)), ((), ())), prefe...  18.9 us
    dot_general x1, matrix products, local(): jnp.einsum('jcr,jcs->crs', centered, centered, precision=highest)  16.9 us
  transfers between devices with their start and end apart: 2, of which 2 were waited for; matrix products, arithmetic and copies ran while one was open for 2% of the time, Pallas kernels for 0%

profile of v1, /device:TPU:0, one launch (start us, length us, event | category | flops | bytes accessed | tf_op | source)
XLA Modules:
  0.0 829.6 jit_solution(14947903450264423572)
XLA Ops:
  7.2 0.0 all-gather.4.cloned.1.call-start
  7.2 0.7 all-gather.4.cloned.1.call-update
  7.9 0.0 all-gather.6.cloned.1.call-start
  7.9 7.5 copy.11
  15.4 128.3 %all_to_all.31 = bf16[512,16,512]{2,0,1:T(8,128)(2,1)} all-to-all(bf16[512,16,512]{2,0,1:T(8,128)(2,1)} %bitcast.28), channel_id=1, replica_groups=mesh['dp_0'=4,'dp_1'=2,'mp_0'=4,'mp_1'=4] {'mp_0','mp_1'}, dimensions={1} | all-to-all | bytes 16777216 | tf_op jit(solution)/shard_map/all_to_all | solution.py:24
  143.8 117.0 %all-gather.4.cloned.1.call-done = bf16[8,192,8192]{2,1,0:T(8,128)(2,1)} async-done(((bf16[8,192,512]{2,1,0:T(8,128)(2,1)}), bf16[8,192,8192]{2,1,0:T(8,128)(2,1)}) %all-gather.4.cloned.1.call-update) | async-done | bytes 25165840 | tf_op jit(solution)/shard_map/all_gather | solution.py:25
  260.8 18.9 %fusion.1 = f32[512,8,192]{0,2,1:T(8,128)S(1)} fusion(bf16[8192,512,1]{1,0,2:T(8,128)(2,1)} %bitcast.30, bf16[8,192,8192]{2,1,0:T(8,128)(2,1)} %all-gather.4.cloned.1.call-done), kind=kOutput, calls=%fused_computation.16 | convolution fusion | flops 12884901888 | bytes 36700160 | tf_op jit(solution)/shard_map/dot_general | solution.py:27
  279.7 0.0 copy-start
  279.7 1.7 copy-done
  281.3 42.7 %all_to_all.32 = f32[512,8,192]{0,2,1:T(8,128)S(1)} all-to-all(f32[512,8,192]{0,2,1:T(8,128)S(1)} %fusion.1), channel_id=1, replica_groups=mesh['dp_0'=4,'dp_1'=2,'mp_0'=4,'mp_1'=4] {'dp_0','dp_1'}, dimensions={1} | all-to-all | bytes 6291456 | tf_op jit(solution)/shard_map/all_to_all | solution.py:40
  324.0 0.3 reduce_sum.77
  324.3 0.6 multiply_reduce_fusion.1
  324.8 16.9 %convolution_convert_fusion = bf16[1536,1536]{1,0:T(8,128)(2,1)} fusion(f32[512,1536]{0,1:T(8,128)S(1)} %bitcast.31), kind=kOutput, calls=%fused_computation.2 | convolution fusion | flops 14497873920 | bytes 7864320 | tf_op jit(solution)/shard_map/jcr,jcs->crs/dot_general | solution.py:48
  341.7 0.0 copy-start.1
  341.7 0.0 all-gather.6.cloned.1.call-update
  341.7 0.7 copy-done.1
  342.4 3.9 convolution_bitcast_fusion
  346.3 0.1 slice_bitcast_fusion.1
  346.3 2.0 multiply_reduce_fusion.2
  349.6 5.4 copy.8
  355.1 0.7 multiply_reduce_fusion.4
  355.7 394.6 %all-gather.6.cloned.1.call-done = bf16[24576,1536]{1,0:T(8,128)(2,1)} async-done(((bf16[1536,1536]{1,0:T(8,128)(2,1)}), bf16[24576,1536]{1,0:T(8,128)(2,1)}) %all-gather.6.cloned.1.call-update) | async-done | bytes 75497488 | tf_op jit(solution)/shard_map/all_gather | solution.py:13
  750.3 26.9 %reduce.8 = bf16[1536,1536]{1,0:T(8,128)(2,1)} reduce(bf16[16,1536,1536]{2,1,0:T(8,128)(2,1)} %bitcast.10, bf16[]{:T(256)} %constant.37.clone.1), dimensions={0}, to_apply=%region_13.14 | reduce | flops 35389440 | bytes 80216064 | tf_op jit(solution)/shard_map/reduce_sum | solution.py:13
  777.3 5.4 multiply_reduce_fusion
  784.1 11.3 %all-reduce.2 = (f32[]{:T(128)}, f32[]{:T(128)}, f32[]{:T(128)}) all-reduce(f32[]{:T(128)S(6)} %add.45, f32[]{:T(128)} %get-tuple-element.9, f32[]{:T(128)S(6)} %sub.61), channel_id=1, replica_groups=mesh['dp_0'=4,'dp_1'=2,'mp_0'=4,'mp_1'=4] {'dp_0'}, use_global_device_ids=true, to_apply=%region_2.0 | all-reduce | flops 3 | bytes 24 | tf_op jit(solution)/shard_map/psum | solution.py:17
  795.3 3.2 all-reduce.3
  798.5 11.1 %all-reduce.1 = (f32[]{:T(128)}, f32[]{:T(128)}, f32[]{:T(128)}) all-reduce(f32[]{:T(128)} %get-tuple-element.19, f32[]{:T(128)} %get-tuple-element.20, f32[]{:T(128)} %get-tuple-element.21), channel_id=1, replica_groups=mesh['dp_0'=4,'dp_1'=2,'mp_0'=4,'mp_1'=4] {'mp_0'}, use_global_device_ids=true, to_apply=%region_4.5 | all-reduce | flops 3 | bytes 24 | tf_op jit(solution)/shard_map/psum | solution.py:17
  809.6 9.3 %all-reduce = (f32[]{:T(128)}, f32[]{:T(128)}, f32[]{:T(128)}) all-reduce(f32[]{:T(128)} %get-tuple-element.13, f32[]{:T(128)} %get-tuple-element.14, f32[]{:T(128)} %get-tuple-element.15), channel_id=1, replica_groups=mesh['dp_0'=4,'dp_1'=2,'mp_0'=4,'mp_1'=4] {'mp_1'}, use_global_device_ids=true, to_apply=%region_5.6 | all-reduce | flops 3 | bytes 24 | tf_op jit(solution)/shard_map/psum | solution.py:17
  822.1 0.6 pad_maximum_fusion
  (1 shorter events, 0.0 us)
Async XLA Ops:
  7.2 253.6 %all-gather.4.cloned.1.call-start = ((), (), s32[]{:S(2)}) async-start(), calls=%async_computation.2 | async-start | bytes 26738688 | tf_op jit(solution)/shard_map/all_gather | solution.py:25
  7.9 742.4 %all-gather.6.cloned.1.call-start = ((), (), s32[]{:S(2)}) async-start(), calls=%async_computation.3 | async-start | bytes 80216064 | tf_op jit(solution)/shard_map/all_gather | solution.py:13
  279.7 1.7 copy-start
  341.7 0.7 copy-start.1
Sparse Core Ops, SparseCore 0:
  10.1 250.6 all-gather.3
  341.8 408.4 all-gather.5
